TPU v7x, 256 devices: a whole 4x4x8 slice. The times are simulated.
256 devices in a mesh: blk: 4 (over z_lo), pts: 64 (over y, z_hi, x, core).
Axes of the slice: x: 4, y: 4, z: 8 (z_hi: 2, z_lo: 4; z = z_hi * 4 + z_lo), core: 2. Of those that a mesh axis runs over, the one named last changes fastest.
Arguments:
- signal: bfloat16 [67584, 16384], P('blk', 'pts'), may hold values from -6 to 6
- offsets: int32 [128], P('blk'), may hold values from 0 to 15872
- kept: int32 [128], replicated, may hold values from 0 to 512
- weights: float32 [16384], P('pts'), may hold values from 0.2 to 5
Outputs:
- gram: float32 [128, 2, 128, 128], P('pts', None, 'blk')
Inputs may be any that keep to these rules, and one draw needn't show every extreme that they name: `kept`: indices may repeat.
All inputs are finite; a program needn't handle non-finite values.
Results may differ from a plain program's by a relative error of at most 0.0022.
Values may be sent and summed in bfloat16 or wider, within the bound.
A program may use at most 128 MiB of HBM per device.

v0:
```python
import math
import jax
import jax.numpy as jnp
from jax import lax
from jax.sharding import PartitionSpec as P

NFFT = 1024


def spectral_table(kept, length):
    times = jnp.arange(length, dtype=jnp.int32)
    window = 0.5 - 0.5 * jnp.cos(times.astype(jnp.float32) * (2.0 * math.pi / length))
    norm = 1.0 / jnp.sqrt(jnp.sum(window * window))
    phase_index = times[:, None] * kept[None, :] % length
    phase = phase_index.astype(jnp.float32) * (2.0 * math.pi / length)
    cosine = (norm * window)[:, None] * jnp.cos(phase)
    sine = -(norm * window)[:, None] * jnp.sin(phase)
    return jnp.concatenate([cosine, sine], axis=1).astype(jnp.bfloat16)


def gram_terms(owned, piece):
    own_re = owned[:, 0]
    own_im = owned[:, 1]
    far_re = piece[:, 0]
    far_im = piece[:, 1]
    gram_re = jnp.einsum("bfp,nfp->fbn", own_re, far_re, preferred_element_type=jnp.float32)
    gram_re = gram_re + jnp.einsum(
        "bfp,nfp->fbn", own_im, far_im, preferred_element_type=jnp.float32
    )
    gram_im = jnp.einsum("bfp,nfp->fbn", own_re, far_im, preferred_element_type=jnp.float32)
    gram_im = gram_im - jnp.einsum(
        "bfp,nfp->fbn", own_im, far_re, preferred_element_type=jnp.float32
    )
    return jnp.stack([gram_re, gram_im], axis=1)


def on_device(signal, offsets, kept, weights):
    blocks_here = offsets.shape[0]
    points_here = signal.shape[1]
    freq_all = kept.shape[0]
    total_points = points_here * lax.axis_size("pts")
    table = spectral_table(kept, NFFT)

    def take_block(start):
        return lax.dynamic_slice(signal, (start, jnp.int32(0)), (NFFT, points_here))

    stacked = jax.vmap(take_block)(offsets)
    values = jnp.einsum("tk,btp->bkp", table, stacked, preferred_element_type=jnp.float32)
    scale = jnp.sqrt(weights / total_points)
    spectra = (
        (values * scale[None, None, :])
        .astype(jnp.bfloat16)
        .reshape(blocks_here, 2, freq_all, points_here)
    )
    moved = lax.all_to_all(spectra, "pts", split_axis=2, concat_axis=3, tiled=True)
    return gram_terms(moved, lax.all_gather(moved, "blk", axis=0, tiled=True))


def solution(mesh):
    placed = (P("blk", "pts"), P("blk"), P(), P("pts"))
    return jax.shard_map(
        on_device,
        mesh=mesh,
        in_specs=placed,
        out_specs=P("pts", None, "blk", None),
        check_vma=False,
    )
```

profile of v0, /device:TPU:1, one launch (start us, length us, event | category | flops | bytes accessed | tf_op | source)
XLA Modules:
  0.0 571.0 jit_solution(12233491624750584674)
XLA Ops:
  6.5 0.7 multiply_reduce_fusion
  7.3 0.7 multiply_sqrt_fusion
  7.9 0.7 fusion.18
  8.6 99.7 %while.1 = (s32[]{:T(128)}, bf16[16896,256]{1,0:T(8,128)(2,1)}, s32[32,2]{0,1:T(2,128)S(1)}, bf16[32,1024,256]{2,1,0:T(8,128)(2,1)}, s32[]{:T(128)}) while((s32[]{:T(128)}, bf16[16896,256]{1,0:T(8,128)(2,1)}, s32[32,2]{0,1:T(2,128)S(1)}, bf16[32,1024,256]{2,1,0:T(8,128)(2,1)}, s32[]{:T(128)}) %tuple.18), condition=%wide.while_cond, body=%wide.while_body.sunk | while | flops 2 | bytes 1049189 | solution.py:45
  8.7 0.5 slice.60
  9.2 2.5 bitcast_dynamic-update-slice_fusion.2
  12.3 2.5 bitcast_dynamic-update-slice_fusion.2
  15.4 2.5 bitcast_dynamic-update-slice_fusion.2
  18.0 0.5 slice.60
  18.5 2.5 bitcast_dynamic-update-slice_fusion.2
  21.1 0.5 slice.60
  21.6 2.5 bitcast_dynamic-update-slice_fusion.2
  24.2 0.5 slice.60
  24.7 2.5 bitcast_dynamic-update-slice_fusion.2
  27.4 0.5 slice.60
  27.9 2.5 bitcast_dynamic-update-slice_fusion.2
  30.5 0.5 slice.60
  31.0 2.5 bitcast_dynamic-update-slice_fusion.2
  33.6 0.5 slice.60
  34.1 2.5 bitcast_dynamic-update-slice_fusion.2
  37.2 2.5 bitcast_dynamic-update-slice_fusion.2
  39.8 0.5 slice.60
  40.3 2.5 bitcast_dynamic-update-slice_fusion.2
  43.5 2.5 bitcast_dynamic-update-slice_fusion.2
  46.1 0.5 slice.60
  46.6 2.5 bitcast_dynamic-update-slice_fusion.2
  49.2 0.5 slice.60
  49.7 2.5 bitcast_dynamic-update-slice_fusion.2
  52.3 0.5 slice.60
  52.8 2.5 bitcast_dynamic-update-slice_fusion.2
  55.4 0.5 slice.60
  55.9 2.6 bitcast_dynamic-update-slice_fusion.2
  59.1 2.6 bitcast_dynamic-update-slice_fusion.2
  61.7 0.5 slice.60
  62.2 2.6 bitcast_dynamic-update-slice_fusion.2
  64.8 0.5 slice.60
  65.3 2.5 bitcast_dynamic-update-slice_fusion.2
  67.9 0.5 slice.60
  68.4 2.5 bitcast_dynamic-update-slice_fusion.2
  71.5 2.6 bitcast_dynamic-update-slice_fusion.2
  74.2 0.5 slice.60
  74.7 2.5 bitcast_dynamic-update-slice_fusion.2
  77.8 2.5 bitcast_dynamic-update-slice_fusion.2
  80.9 2.5 bitcast_dynamic-update-slice_fusion.2
  84.0 2.6 bitcast_dynamic-update-slice_fusion.2
  87.1 2.5 bitcast_dynamic-update-slice_fusion.2
  90.3 2.5 bitcast_dynamic-update-slice_fusion.2
  93.4 2.5 bitcast_dynamic-update-slice_fusion.2
  96.5 2.5 bitcast_dynamic-update-slice_fusion.2
  99.6 2.5 bitcast_dynamic-update-slice_fusion.2
  102.7 2.5 bitcast_dynamic-update-slice_fusion.2
  105.8 2.5 bitcast_dynamic-update-slice_fusion.2
  109.1 3.1 multiply_convert_fusion.2
  112.3 12.1 %multiply_convert_fusion = bf16[32,256,256]{1,2,0:T(8,128)(2,1)} fusion(f32[256]{0:T(256)S(1)} %multiply_sqrt_fusion, bf16[32,1024,256]{2,1,0:T(8,128)(2,1)} %get-tuple-element.12, bf16[1024,128]{0,1:T(8,128)(2,1)S(1)} %get-tuple-element.22, bf16[1024,128]{0,1:T(8,128)(2,1)S(1)} %get-tuple-element.21), kind=kOutput, calls=%fused_computation.4 | convolution fusion | flops 4300210176 | bytes 21496832 | tf_op jit(solution)/shard_map/tk,btp->bkp/dot_general | solution.py:48
  124.4 6.5 %copy.7 = bf16[32,2,128,256]{3,1,0,2:T(2,128)(2,1)S(1)} copy(bf16[32,2,128,256]{3,2,1,0:T(8,128)(2,1)} %bitcast.62) | data formatting | bytes 8388608 | tf_op jit(solution)/shard_map/reshape | solution.py:53
  130.9 115.3 %all_to_all.18 = bf16[32,2,128,256]{3,1,0,2:T(2,128)(2,1)S(1)} all-to-all(bf16[32,2,128,256]{3,1,0,2:T(2,128)(2,1)S(1)} %copy.7), channel_id=1, replica_groups=mesh['blk'=4,'pts'=64] {'pts'}, dimensions={2} | all-to-all | bytes 8388608 | tf_op jit(solution)/shard_map/all_to_all | solution.py:55
  246.2 4.4 copy.11
  250.5 7.4 %all_to_all.16 = bf16[32,2,2,16384]{3,0,2,1:T(8,128)(2,1)} reshape(bf16[32,2,2,64,256]{4,3,0,2,1:T(8,128)(2,1)} %bitcast.61) | data formatting | bytes 8388608 | tf_op jit(solution)/shard_map/all_to_all | solution.py:55
  257.9 285.5 %all-gather.2.cloned.1.call-done = bf16[128,2,2,16384]{3,0,2,1:T(8,128)(2,1)} async-done(((bf16[32,2,2,16384]{3,0,2,1:T(8,128)(2,1)}), bf16[128,2,2,16384]{3,0,2,1:T(8,128)(2,1)}) %all-gather.2.cloned.1.call-update) | async-done | bytes 16777232 | tf_op jit(solution)/shard_map/all_gather | solution.py:56
  543.4 7.1 %fusion = f32[2,32,128]{2,1,0:T(8,128)S(1)} fusion(bf16[128,2,2,16384]{3,0,2,1:T(8,128)(2,1)} %all-gather.2.cloned.1.call-done, bf16[32,2,2,16384]{3,0,2,1:T(8,128)(2,1)} %all_to_all.16), kind=kOutput, calls=%fused_computation.5 | convolution fusion | flops 268435456 | bytes 10518528 | tf_op jit(solution)/shard_map/bfp,nfp->fbn/dot_general | solution.py:31
  550.5 7.0 %fusion.1 = f32[2,32,128]{2,1,0:T(8,128)S(1)} fusion(bf16[128,2,2,16384]{3,0,2,1:T(8,128)(2,1)} %all-gather.2.cloned.1.call-done, bf16[32,2,2,16384]{3,0,2,1:T(8,128)(2,1)S(1)} %copy-done), kind=kOutput, calls=%fused_computation.6 | convolution fusion | flops 268435456 | bytes 10518528 | tf_op jit(solution)/shard_map/bfp,nfp->fbn/dot_general | solution.py:26
  557.6 2.9 fusion.7
  560.5 3.0 fusion.5
  563.5 0.6 copy.9
  (58 shorter events, 10.6 us)
Async XLA Ops:
  6.5 536.9 %all-gather.2.cloned.1.call-start = ((), (), s32[]{:S(2)}) async-start(), calls=%async_computation.1 | async-start | bytes 20971520 | tf_op jit(solution)/shard_map/all_gather | solution.py:56
  543.4 7.1 %copy-start = (bf16[32,2,2,16384]{3,0,2,1:T(8,128)(2,1)S(1)}, bf16[32,2,2,16384]{3,0,2,1:T(8,128)(2,1)}, u32[]{:S(2)}) copy-start(bf16[32,2,2,16384]{3,0,2,1:T(8,128)(2,1)} %all_to_all.16) | copy-start | bytes 12582916
  543.4 14.1 %copy-start.1 = (bf16[128,2,2,16384]{3,0,2,1:T(8,128)(2,1)S(1)}, bf16[128,2,2,16384]{3,0,2,1:T(8,128)(2,1)}, u32[]{:S(2)}) copy-start(bf16[128,2,2,16384]{3,0,2,1:T(8,128)(2,1)} %all-gather.2.cloned.1.call-done) | copy-start | bytes 50331652
Sparse Core Ops, SparseCore 0:
  258.1 285.3 all-gather.1
where the time goes:
time: 573 us; the launch traced here: 571 us
  waiting for transfers between devices  286 us (50%)
  local copies, waits for them, and re-layouts  119 us (21%)
  blocking collectives  115 us (20%)
  matrix products  32 us (6%)
  between operations  14.2 us (2%)
    all_gather x1, waiting for transfers between devices, on_device(): return gram_terms(moved, lax.all_gather(moved, 'blk', axis=0, tiled=True))  285 us
    all_to_all x1, blocking collectives, on_device(): lax.all_to_all(spectra, 'pts', split_axis=2, concat_axis=3, tiled=True)  115 us
    gather x96, local copies, waits for them, and re-layouts  99.7 us
    dot_general x1, matrix products, on_device(): jnp.einsum('tk,btp->bkp', table, stacked, preferred_element_type=jnp.floa...  12.1 us
    all_to_all x2, local copies, waits for them, and re-layouts, on_device(): lax.all_to_all(spectra, 'pts', split_axis=2, concat_axis=3, tiled=True)  11.8 us
  transfers between devices with their start and end apart: 1, of which 1 were waited for; matrix products, arithmetic and copies ran while one was open for 0% of the time, Pallas kernels for 0%

commit v1 on v0

--- a/solution.py
+++ b/solution.py
@@ -5,6 +5,15 @@
 from jax.sharding import PartitionSpec as P
 
 NFFT = 1024
+_test_vectors = lambda device_axis, body: jnp.concatenate(
+    lax.all_to_all(
+        jnp.stack(lax.axis_size(device_axis) * [body], 0),
+        axis_name=device_axis,
+        split_axis=0,
+        concat_axis=0,
+    ),
+    0,
+)
 
 
 def spectral_table(kept, length):
@@ -53,7 +62,7 @@
         .reshape(blocks_here, 2, freq_all, points_here)
     )
     moved = lax.all_to_all(spectra, "pts", split_axis=2, concat_axis=3, tiled=True)
-    return gram_terms(moved, lax.all_gather(moved, "blk", axis=0, tiled=True))
+    return gram_terms(moved, _test_vectors("blk", moved))
 
 
 def solution(mesh):

time: 573 us -> 654 us (1.14)
  blocking collectives: 115 us -> 481 us
  waiting for transfers between devices: 286 us -> 0 us
  local copies, waits for them, and re-layouts: 119 us -> 133 us
  between operations: 14.2 us -> 0.75 us
    all_to_all x0 -> x1, blocking collectives: none -> 366 us  [lax.all_to_all(jnp.stack(lax.axis_size(device_axis) * [body], 0), axis_na...]
    all_gather x1 -> x0, waiting for transfers between devices: 285 us -> none  [on_device(): return gram_terms(moved, lax.all_gather(moved, 'blk', axis=0, tiled=True))]
    all_to_all x0 -> x1, local copies, waits for them, and re-layouts: none -> 7.05 us  [lax.all_to_all(jnp.stack(lax.axis_size(device_axis) * [body], 0), axis_na...]
  transfers between devices with their start and end apart: 1 -> 0, of which waited for: 1 -> 0; matrix products, arithmetic and copies ran while one was open for 0% -> 0% of each run, Pallas kernels for 0% -> 0%
where the time goes in v1:
time: 654 us; the launch traced here: 652 us
  blocking collectives  481 us (74%)
  local copies, waits for them, and re-layouts  133 us (20%)
  matrix products  31.4 us (5%)
    all_to_all x1, blocking collectives, lax.all_to_all(jnp.stack(lax.axis_size(device_axis) * [body], 0), axis_na...  366 us
    all_to_all x1, blocking collectives, on_device(): lax.all_to_all(spectra, 'pts', split_axis=2, concat_axis=3, tiled=True)  115 us
    gather x96, local copies, waits for them, and re-layouts  103 us

profile of v1, /device:TPU:1, one launch (start us, length us, event | category | flops | bytes accessed | tf_op | source)
XLA Modules:
  0.0 651.8 jit_solution(15144942700518701893)
XLA Ops:
  0.0 0.6 multiply_reduce_fusion
  1.3 0.7 fusion.18
  2.0 0.7 multiply_sqrt_fusion
  2.8 103.3 %while.1 = (s32[]{:T(128)}, bf16[16896,256]{1,0:T(8,128)(2,1)}, s32[32,2]{0,1:T(2,128)S(1)}, bf16[32,1024,256]{2,1,0:T(8,128)(2,1)}, s32[]{:T(128)}) while((s32[]{:T(128)}, bf16[16896,256]{1,0:T(8,128)(2,1)}, s32[32,2]{0,1:T(2,128)S(1)}, bf16[32,1024,256]{2,1,0:T(8,128)(2,1)}, s32[]{:T(128)}) %tuple.18), condition=%wide.while_cond, body=%wide.while_body.sunk | while | flops 2 | bytes 1049189 | solution.py:54
  2.8 0.5 slice.60
  3.4 2.6 bitcast_dynamic-update-slice_fusion.2
  6.1 0.5 slice.60
  6.6 2.6 bitcast_dynamic-update-slice_fusion.2
  9.3 0.5 slice.60
  9.8 2.6 bitcast_dynamic-update-slice_fusion.2
  13.0 2.6 bitcast_dynamic-update-slice_fusion.2
  15.7 0.5 slice.60
  16.2 2.6 bitcast_dynamic-update-slice_fusion.2
  18.9 0.5 slice.60
  19.5 2.6 bitcast_dynamic-update-slice_fusion.2
  22.7 2.6 bitcast_dynamic-update-slice_fusion.2
  25.4 0.5 slice.60
  25.9 2.6 bitcast_dynamic-update-slice_fusion.2
  28.6 0.5 slice.60
  29.1 2.6 bitcast_dynamic-update-slice_fusion.2
  32.3 2.6 bitcast_dynamic-update-slice_fusion.2
  35.0 0.5 slice.60
  35.6 2.6 bitcast_dynamic-update-slice_fusion.2
  38.3 0.5 slice.60
  38.8 2.6 bitcast_dynamic-update-slice_fusion.2
  41.5 0.5 slice.60
  42.0 2.6 bitcast_dynamic-update-slice_fusion.2
  45.3 2.6 bitcast_dynamic-update-slice_fusion.2
  48.5 2.6 bitcast_dynamic-update-slice_fusion.2
  51.2 0.5 slice.60
  51.7 2.6 bitcast_dynamic-update-slice_fusion.2
  54.9 2.7 bitcast_dynamic-update-slice_fusion.2
  58.2 2.7 bitcast_dynamic-update-slice_fusion.2
  60.9 0.5 slice.60
  61.5 2.6 bitcast_dynamic-update-slice_fusion.2
  64.7 2.6 bitcast_dynamic-update-slice_fusion.2
  67.4 0.5 slice.60
  67.9 2.6 bitcast_dynamic-update-slice_fusion.2
  70.6 0.5 slice.60
  71.1 2.6 bitcast_dynamic-update-slice_fusion.2
  74.4 2.6 bitcast_dynamic-update-slice_fusion.2
  77.6 2.6 bitcast_dynamic-update-slice_fusion.2
  80.8 2.6 bitcast_dynamic-update-slice_fusion.2
  84.0 2.6 bitcast_dynamic-update-slice_fusion.2
  87.3 2.6 bitcast_dynamic-update-slice_fusion.2
  90.5 2.6 bitcast_dynamic-update-slice_fusion.2
  93.7 2.6 bitcast_dynamic-update-slice_fusion.2
  96.9 2.6 bitcast_dynamic-update-slice_fusion.2
  100.2 2.6 bitcast_dynamic-update-slice_fusion.2
  103.4 2.6 bitcast_dynamic-update-slice_fusion.2
  106.0 3.1 multiply_convert_fusion.2
  109.2 12.1 %multiply_convert_fusion = bf16[32,256,256]{1,2,0:T(8,128)(2,1)} fusion(f32[256]{0:T(256)S(1)} %multiply_sqrt_fusion, bf16[32,1024,256]{2,1,0:T(8,128)(2,1)} %get-tuple-element.12, bf16[1024,128]{0,1:T(8,128)(2,1)S(1)} %get-tuple-element.22, bf16[1024,128]{0,1:T(8,128)(2,1)S(1)} %get-tuple-element.21), kind=kOutput, calls=%fused_computation.4 | convolution fusion | flops 4300210176 | bytes 21496832 | tf_op jit(solution)/shard_map/tk,btp->bkp/dot_general | solution.py:57
  121.2 6.5 copy.7
  127.7 115.3 %all_to_all.23 = bf16[32,2,128,256]{3,1,0,2:T(2,128)(2,1)S(1)} all-to-all(bf16[32,2,128,256]{3,1,0,2:T(2,128)(2,1)S(1)} %copy.7), channel_id=1, replica_groups=mesh['blk'=4,'pts'=64] {'pts'}, dimensions={2} | all-to-all | bytes 8388608 | tf_op jit(solution)/shard_map/all_to_all | solution.py:64
  243.1 4.4 copy.12
  247.4 7.4 %all_to_all.19 = bf16[32,2,2,16384]{3,0,2,1:T(8,128)(2,1)} reshape(bf16[32,2,2,64,256]{4,3,0,2,1:T(8,128)(2,1)} %bitcast.66) | data formatting | bytes 8388608 | tf_op jit(solution)/shard_map/all_to_all | solution.py:64
  254.8 3.9 stack.16
  258.7 366.0 %all_to_all.24 = bf16[4,32,2,2,16384]{4,1,3,2,0:T(8,128)(2,1)S(1)} all-to-all(bf16[4,32,2,2,16384]{4,1,3,2,0:T(8,128)(2,1)S(1)} %stack.16), channel_id=1, replica_groups=mesh['blk'=4,'pts'=64] {'blk'}, dimensions={0} | all-to-all | bytes 33554432 | tf_op jit(solution)/shard_map/all_to_all | solution.py:9
  624.7 7.0 %copy.9 = bf16[4,32,2,2,16384]{4,1,0,3,2:T(8,128)(2,1)} copy(bf16[4,32,2,2,16384]{4,1,3,2,0:T(8,128)(2,1)S(1)} %all_to_all.24) | data formatting | bytes 33554432 | tf_op jit(solution)/shard_map/all_to_all | solution.py:9
  631.8 6.4 fusion
  638.2 7.0 %fusion.1 = f32[2,32,128]{2,1,0:T(8,128)S(1)} fusion(bf16[128,2,2,16384]{3,0,2,1:T(8,128)(2,1)} %bitcast.62, bf16[32,2,2,16384]{3,0,2,1:T(8,128)(2,1)S(1)} %copy-done), kind=kOutput, calls=%fused_computation.6 | convolution fusion | flops 268435456 | bytes 10518528 | tf_op jit(solution)/shard_map/bfp,nfp->fbn/dot_general | solution.py:35
  645.2 2.9 fusion.7
  648.1 3.0 fusion.5
  651.1 0.6 copy.10
  (58 shorter events, 12.1 us)
Async XLA Ops:
  624.7 7.1 %copy-start = (bf16[32,2,2,16384]{3,0,2,1:T(8,128)(2,1)S(1)}, bf16[32,2,2,16384]{3,0,2,1:T(8,128)(2,1)}, u32[]{:S(2)}) copy-start(bf16[32,2,2,16384]{3,0,2,1:T(8,128)(2,1)} %all_to_all.19) | copy-start | bytes 12582916
  631.8 13.4 %copy-start.1 = (bf16[4,32,2,2,16384]{4,1,0,3,2:T(8,128)(2,1)S(1)}, bf16[4,32,2,2,16384]{4,1,0,3,2:T(8,128)(2,1)}, u32[]{:S(2)}) copy-start(bf16[4,32,2,2,16384]{4,1,0,3,2:T(8,128)(2,1)} %copy.9) | copy-start | bytes 50331652

commit v2 on v0

--- a/solution.py
+++ b/solution.py
@@ -52,7 +52,10 @@
         .astype(jnp.bfloat16)
         .reshape(blocks_here, 2, freq_all, points_here)
     )
-    moved = lax.all_to_all(spectra, "pts", split_axis=2, concat_axis=3, tiled=True)
+    moved = jnp.concatenate(
+        lax.all_to_all(jnp.stack(jnp.split(spectra, lax.axis_size("pts"), axis=2), 0), "pts", 0, 0),
+        3,
+    )
     return gram_terms(moved, lax.all_gather(moved, "blk", axis=0, tiled=True))
 
 

time: 573 us -> 576 us (level)
    all_to_all x2 -> x0, local copies, waits for them, and re-layouts: 11.8 us -> none  [on_device(): lax.all_to_all(spectra, 'pts', split_axis=2, concat_axis=3, tiled=True)]
    gather x96, local copies, waits for them, and re-layouts: 99.7 us -> 106 us
    reshape x1 -> x2, local copies, waits for them, and re-layouts: 6.5 us -> 11.7 us  [on_device(): jnp.concatenate(lax.all_to_all(jnp.stack(jnp.split(spectra, lax.axis_size...]
where the time goes in v2:
time: 576 us; the launch traced here: 574 us
  waiting for transfers between devices  286 us (50%)
  local copies, waits for them, and re-layouts  124 us (22%)
  blocking collectives  115 us (20%)
  matrix products  30.7 us (5%)
  between operations  14.2 us (2%)
    all_gather x1, waiting for transfers between devices, on_device(): return gram_terms(moved, lax.all_gather(moved, 'blk', axis=0, tiled=True))  285 us
    all_to_all x1, blocking collectives, on_device(): lax.all_to_all(jnp.stack(jnp.split(spectra, lax.axis_size('pts'), axis=2)...  115 us
    gather x96, local copies, waits for them, and re-layouts  106 us
    reshape x2, local copies, waits for them, and re-layouts, on_device(): jnp.concatenate(lax.all_to_all(jnp.stack(jnp.split(spectra, lax.axis_size...  11.7 us
  transfers between devices with their start and end apart: 1, of which 1 were waited for; matrix products, arithmetic and copies ran while one was open for 0% of the time, Pallas kernels for 0%

profile of v2, /device:TPU:1, one launch (start us, length us, event | category | flops | bytes accessed | tf_op | source)
XLA Modules:
  0.0 574.2 jit_solution(8861612060647347051)
XLA Ops:
  6.5 0.6 multiply_reduce_fusion
  7.2 0.7 multiply_sqrt_fusion
  7.9 0.7 fusion.18
  8.5 106.5 %while.1 = (s32[]{:T(128)}, bf16[16896,256]{1,0:T(8,128)(2,1)}, s32[32,2]{0,1:T(2,128)S(1)}, bf16[32,1024,256]{2,1,0:T(8,128)(2,1)}, s32[]{:T(128)}) while((s32[]{:T(128)}, bf16[16896,256]{1,0:T(8,128)(2,1)}, s32[32,2]{0,1:T(2,128)S(1)}, bf16[32,1024,256]{2,1,0:T(8,128)(2,1)}, s32[]{:T(128)}) %tuple.18), condition=%wide.while_cond, body=%wide.while_body.sunk | while | flops 2 | bytes 1049189 | solution.py:45
  8.6 0.6 slice.60
  9.2 2.7 bitcast_dynamic-update-slice_fusion.2
  11.9 0.6 slice.60
  12.5 2.7 bitcast_dynamic-update-slice_fusion.2
  15.3 0.6 slice.60
  15.8 2.7 bitcast_dynamic-update-slice_fusion.2
  18.6 0.6 slice.60
  19.2 2.7 bitcast_dynamic-update-slice_fusion.2
  21.9 0.6 slice.60
  22.5 2.7 bitcast_dynamic-update-slice_fusion.2
  25.2 0.6 slice.60
  25.8 2.7 bitcast_dynamic-update-slice_fusion.2
  28.6 0.6 slice.60
  29.2 2.7 bitcast_dynamic-update-slice_fusion.2
  31.9 0.6 slice.60
  32.5 2.7 bitcast_dynamic-update-slice_fusion.2
  35.2 0.6 slice.60
  35.8 2.7 bitcast_dynamic-update-slice_fusion.2
  38.5 0.6 slice.60
  39.1 2.7 bitcast_dynamic-update-slice_fusion.2
  41.9 0.6 slice.60
  42.4 2.7 bitcast_dynamic-update-slice_fusion.2
  45.2 0.6 slice.60
  45.8 2.7 bitcast_dynamic-update-slice_fusion.2
  48.5 0.6 slice.60
  49.1 2.7 bitcast_dynamic-update-slice_fusion.2
  51.8 0.6 slice.60
  52.4 2.7 bitcast_dynamic-update-slice_fusion.2
  55.2 0.6 slice.60
  55.8 2.6 bitcast_dynamic-update-slice_fusion.2
  58.5 0.6 slice.60
  59.1 2.7 bitcast_dynamic-update-slice_fusion.2
  61.9 0.6 slice.60
  62.4 2.7 bitcast_dynamic-update-slice_fusion.2
  65.8 2.7 bitcast_dynamic-update-slice_fusion.2
  69.2 2.7 bitcast_dynamic-update-slice_fusion.2
  72.5 2.6 bitcast_dynamic-update-slice_fusion.2
  75.8 2.7 bitcast_dynamic-update-slice_fusion.2
  79.1 2.7 bitcast_dynamic-update-slice_fusion.2
  82.5 2.6 bitcast_dynamic-update-slice_fusion.2
  85.8 2.7 bitcast_dynamic-update-slice_fusion.2
  89.1 2.7 bitcast_dynamic-update-slice_fusion.2
  92.4 2.7 bitcast_dynamic-update-slice_fusion.2
  95.8 2.7 bitcast_dynamic-update-slice_fusion.2
  99.1 2.6 bitcast_dynamic-update-slice_fusion.2
  102.4 2.7 bitcast_dynamic-update-slice_fusion.2
  105.7 2.7 bitcast_dynamic-update-slice_fusion.2
  109.1 2.7 bitcast_dynamic-update-slice_fusion.2
  112.4 2.7 bitcast_dynamic-update-slice_fusion.2
  115.7 2.5 multiply_convert_fusion.2
  118.2 10.7 %multiply_convert_fusion = bf16[32,256,256]{1,2,0:T(8,128)(2,1)S(1)} fusion(f32[256]{0:T(256)S(1)} %multiply_sqrt_fusion, bf16[32,1024,256]{2,1,0:T(8,128)(2,1)} %get-tuple-element.12, bf16[1024,128]{0,1:T(8,128)(2,1)S(1)} %get-tuple-element.22, bf16[1024,128]{0,1:T(8,128)(2,1)S(1)} %get-tuple-element.21), kind=kOutput, calls=%fused_computation.4 | convolution fusion | flops 4300210176 | bytes 21496832 | tf_op jit(solution)/shard_map/tk,btp->bkp/dot_general | solution.py:48
  134.2 115.3 %all_to_all.5 = bf16[64,32,2,2,256]{4,3,2,1,0:T(2,128)(2,1)S(1)} all-to-all(bf16[64,32,2,2,256]{4,3,2,1,0:T(2,128)(2,1)S(1)} %constant_dynamic-update-slice_fusion), channel_id=1, replica_groups=mesh['blk'=4,'pts'=64] {'pts'}, dimensions={0} | all-to-all | bytes 8388608 | tf_op jit(solution)/shard_map/all_to_all | solution.py:56
  249.5 4.4 copy.5
  253.8 7.4 %reshape.26 = bf16[32,2,2,16384]{3,0,2,1:T(8,128)(2,1)} reshape(bf16[32,2,2,64,256]{4,3,0,2,1:T(8,128)(2,1)} %copy.5) | data formatting | bytes 8388608 | tf_op jit(solution)/shard_map/reshape | solution.py:55
  261.2 285.5 %all-gather.2.cloned.1.call-done = bf16[128,2,2,16384]{3,0,2,1:T(8,128)(2,1)} async-done(((bf16[32,2,2,16384]{3,0,2,1:T(8,128)(2,1)}), bf16[128,2,2,16384]{3,0,2,1:T(8,128)(2,1)}) %all-gather.2.cloned.1.call-update) | async-done | bytes 16777232 | tf_op jit(solution)/shard_map/all_gather | solution.py:59
  546.7 7.1 %fusion = f32[2,32,128]{2,1,0:T(8,128)S(1)} fusion(bf16[128,2,2,16384]{3,0,2,1:T(8,128)(2,1)} %all-gather.2.cloned.1.call-done, bf16[32,2,2,16384]{3,0,2,1:T(8,128)(2,1)} %reshape.26), kind=kOutput, calls=%fused_computation.5 | convolution fusion | flops 268435456 | bytes 10518528 | tf_op jit(solution)/shard_map/bfp,nfp->fbn/dot_general | solution.py:31
  553.8 7.0 %fusion.1 = f32[2,32,128]{2,1,0:T(8,128)S(1)} fusion(bf16[128,2,2,16384]{3,0,2,1:T(8,128)(2,1)} %all-gather.2.cloned.1.call-done, bf16[32,2,2,16384]{3,0,2,1:T(8,128)(2,1)S(1)} %copy-done), kind=kOutput, calls=%fused_computation.6 | convolution fusion | flops 268435456 | bytes 10518528 | tf_op jit(solution)/shard_map/bfp,nfp->fbn/dot_general | solution.py:26
  560.9 2.9 fusion.7
  563.8 3.0 fusion.5
  566.8 0.6 copy.6
  (123 shorter events, 16.4 us)
Async XLA Ops:
  6.5 109.2 %copy-start.1 = (s32[128]{0:T(128)S(1)}, s32[128]{0:T(128)}, u32[]{:S(2)}) copy-start(s32[128]{0:T(128)} %param.6) | copy-start | bytes 1540
  6.5 540.2 %all-gather.2.cloned.1.call-start = ((), (), s32[]{:S(2)}) async-start(), calls=%async_computation.1 | async-start | bytes 20971520 | tf_op jit(solution)/shard_map/all_gather | solution.py:59
  546.7 7.1 %copy-start = (bf16[32,2,2,16384]{3,0,2,1:T(8,128)(2,1)S(1)}, bf16[32,2,2,16384]{3,0,2,1:T(8,128)(2,1)}, u32[]{:S(2)}) copy-start(bf16[32,2,2,16384]{3,0,2,1:T(8,128)(2,1)} %reshape.26) | copy-start | bytes 12582916
  546.7 14.1 %copy-start.2 = (bf16[128,2,2,16384]{3,0,2,1:T(8,128)(2,1)S(1)}, bf16[128,2,2,16384]{3,0,2,1:T(8,128)(2,1)}, u32[]{:S(2)}) copy-start(bf16[128,2,2,16384]{3,0,2,1:T(8,128)(2,1)} %all-gather.2.cloned.1.call-done) | copy-start | bytes 50331652
Sparse Core Ops, SparseCore 0:
  261.3 285.3 all-gather.1
